TPU v7x, 32 devices: a whole 2x2x4 slice. The times are simulated.
32 devices in a mesh: expert: 8 (over z, y), tensor: 4 (over x, core).
Axes of the slice: x: 2, y: 2, z: 4, core: 2. Of those that a mesh axis runs over, the one named last changes fastest.
Arguments:
- tokens: bfloat16 [1024, 2880], P(('expert', 'tensor')), may hold values from -6 to 6
- cotangent: bfloat16 [1024, 2880], P(('expert', 'tensor')), may hold values from -6 to 6
- routes: int32 [1024, 4], P(('expert', 'tensor')), may hold values from 0 to 7, all different within a row; in each aligned block of 32 rows (0 to 31, 32 to 63, ...) at most 24 rows name the same one
- combine: float32 [1024, 4], P(('expert', 'tensor')), may hold values from 0.1 to 1
- w_gate: bfloat16 [8, 2880, 1440], P('expert', None, 'tensor'), may hold values from -0.109375 to 0.109375
- w_up: bfloat16 [8, 2880, 1440], P('expert', None, 'tensor'), may hold values from -0.109375 to 0.109375
- w_down: bfloat16 [8, 1440, 2880], P('expert', 'tensor'), may hold values from -0.15625 to 0.15625
Outputs:
- token_grad: bfloat16 [1024, 2880], P(('expert', 'tensor'))
- gate_grad: bfloat16 [8, 2880, 1440], P('expert', None, 'tensor')
- up_grad: bfloat16 [8, 2880, 1440], P('expert', None, 'tensor')
- down_grad: bfloat16 [8, 1440, 2880], P('expert', 'tensor')
Inputs may be any that keep to these rules, and one draw needn't show every extreme that they name: `routes`: each row names 4 different experts. Among the rows of one device no expert is named more than 24 times, and in every draw some expert is named exactly 24 times by the rows of some device.
All inputs are finite; a program needn't handle non-finite values.
Results may differ from a plain program's by a relative error of at most 0.0065.
Values may be sent and summed in bfloat16 or wider, within the bound.
A program may use at most 128 MiB of HBM per device.

v0:
```python
import jax
import jax.numpy as jnp
from jax import lax
from jax.experimental import pallas as pl
from jax.experimental.pallas import tpu as pltpu
from jax.sharding import PartitionSpec as P

MESH = pl.DeviceIdType.MESH


def route_slots(flat, experts, cap):
    onehot = (flat[:, None] == jnp.arange(experts, dtype=jnp.int32)[None, :]).astype(jnp.int32)
    before = jnp.cumsum(onehot, axis=0) - onehot
    place = jnp.sum(before * onehot, axis=1)
    return flat * cap + place


def contract_rows(left, right):
    return lax.dot_general(
        left, right, (((0,), (0,)), ((), ())), preferred_element_type=jnp.float32
    )


def contract_cols(left, right):
    return lax.dot_general(
        left, right, (((1,), (1,)), ((), ())), preferred_element_type=jnp.float32
    )


def slotted(tokens, cotangent, routes, combine, w_gate, w_up, w_down):
    tok_rows, width = tokens.shape
    top_count = routes.shape[1]
    groups = lax.axis_size("expert")
    experts = groups * w_gate.shape[0]
    cap = max(2, 3 * tok_rows * top_count // (2 * experts))
    flat = routes.reshape(-1)
    slot = route_slots(flat, experts, cap)
    target = jnp.arange(experts * cap, dtype=jnp.int32)
    match = slot[None, :] == target[:, None]
    valid = jnp.any(match, axis=1)
    order = jnp.arange(flat.shape[0], dtype=jnp.int32)
    source = jnp.sum(jnp.where(match, order[None, :], 0), axis=1)
    token = source // top_count
    send_x = jnp.where(valid[:, None], tokens[token], jnp.zeros((), tokens.dtype))
    scaled = combine.reshape(-1)[source][:, None] * cotangent[token].astype(jnp.float32)
    send_dy = jnp.where(valid[:, None], scaled, 0.0).astype(jnp.bfloat16)
    send_x = send_x.reshape(groups, cap, width)
    send_dy = send_dy.reshape(groups, cap, width)
    recv_x, recv_dy = (
        lax.all_to_all(send_x, "expert", split_axis=0, concat_axis=0, tiled=True),
        lax.all_to_all(send_dy, "expert", split_axis=0, concat_axis=0, tiled=True),
    )
    recv_x = recv_x.reshape(groups * cap, width)
    recv_dy = recv_dy.reshape(groups * cap, width)
    xs, dys = (
        lax.all_gather(recv_x, "tensor", axis=0, tiled=True),
        lax.all_gather(recv_dy, "tensor", axis=0, tiled=True),
    )
    gate_w = w_gate[0]
    up_w = w_up[0]
    down_w = w_down[0]
    gate = jnp.dot(xs, gate_w, preferred_element_type=jnp.float32)
    upper = jnp.dot(xs, up_w, preferred_element_type=jnp.float32)
    sigma = jax.nn.sigmoid(gate)
    act = (gate * sigma * upper).astype(jnp.bfloat16)
    d_act = contract_cols(dys, down_w)
    down_grad = contract_rows(act, dys).astype(jnp.bfloat16)
    d_upper = (d_act * gate * sigma).astype(jnp.bfloat16)
    d_gate = (d_act * upper * sigma * (1.0 + gate * (1.0 - sigma))).astype(jnp.bfloat16)
    gate_grad = contract_rows(xs, d_gate).astype(jnp.bfloat16)
    up_grad = contract_rows(xs, d_upper).astype(jnp.bfloat16)
    own = lax.psum_scatter(
        contract_cols(d_gate, gate_w) + contract_cols(d_upper, up_w),
        "tensor",
        scatter_dimension=0,
        tiled=True,
    )
    own = own.astype(jnp.bfloat16).reshape(groups, cap, width)
    back = lax.all_to_all(own, "expert", split_axis=0, concat_axis=0, tiled=True).reshape(
        experts * cap, width
    )
    picked = back[slot].astype(jnp.float32).reshape(tok_rows, top_count, width)
    token_grad = jnp.sum(picked, axis=1).astype(jnp.bfloat16)
    return (token_grad, gate_grad[None], up_grad[None], down_grad[None])


def place():
    e, t = lax.axis_index("expert"), lax.axis_index("tensor")
    return e // 2, lax.rem(e, 2), t // 2, lax.rem(t, 2)


def peers(depth):
    z, y, x, c = place()
    e, t = z * 2 + y, x * 2 + c
    along = [(lax.rem(z + step, depth) * 2 + y, t) for step in range(1, depth)]
    return along, (z * 2 + 1 - y, t), (e, (1 - x) * 2 + c), (e, x * 2 + 1 - c)


def greet(depth):
    along, over_y, over_x, twin = peers(depth)
    barrier = pltpu.get_barrier_semaphore()
    for device in [*along, over_y, over_x, twin]:
        pl.semaphore_signal(barrier, inc=1, device_id=device, device_id_type=MESH)
    pl.semaphore_wait(barrier, depth + 2)


def gather_kernel(depth, s_in, x_in, d_in, s_out, x_out, d_out, send_sem, recv_sem, local_sem):
    z, y, x, c = place()
    along, over_y, over_x, twin = peers(depth)
    ins, outs = (s_in, x_in, d_in), (s_out, x_out, d_out)
    sent = [[], [], []]

    def block(dz, dy, dx, dc=0):
        zz = lax.rem(z + dz, depth)
        yy, xx, cc = (1 - y if dy else y), (1 - x if dx else x), (1 - c if dc else c)
        return (zz * 2 + yy) * 4 + xx * 2 + cc

    def send(p, at, device, first=False):
        copy = pltpu.make_async_remote_copy(
            src_ref=ins[p] if first else outs[p].at[at],
            dst_ref=outs[p].at[at],
            send_sem=send_sem.at[p, len(sent[p])],
            recv_sem=recv_sem.at[p, at],
            device_id=device,
            device_id_type=MESH,
        )
        copy.start()
        sent[p].append(copy)

    def landed(p, at):
        pltpu.make_async_remote_copy(
            src_ref=ins[p],
            dst_ref=outs[p].at[at],
            send_sem=send_sem.at[p, 0],
            recv_sem=recv_sem.at[p, at],
            device_id=twin,
            device_id_type=MESH,
        ).wait_recv()

    me = block(0, 0, 0)
    keep = [pltpu.make_async_copy(ins[p], outs[p].at[me], local_sem.at[p]) for p in range(3)]
    for copy in keep:
        copy.start()
    greet(depth)
    for device in [over_y, over_x, *along, twin]:
        for p in range(3):
            send(p, me, device, True)

    def first_level(dz):
        at = block(dz, 0, 0)
        for p in range(3):
            landed(p, at)
            for device in (over_x, over_y, twin):
                send(p, at, device)

    def second_level(dz):
        by_y, by_x = block(dz, 1, 0), block(dz, 0, 1)
        for p in range(3):
            near, far, onward = (by_x, by_y, over_y) if p == 2 else (by_y, by_x, over_x)
            landed(p, near)
            send(p, near, onward)
            send(p, near, twin)
            landed(p, far)
            send(p, far, twin)

    for dz in range(1, depth):
        first_level(dz)
        second_level(dz - 1)
    second_level(depth - 1)
    for dz in range(depth):
        at = block(dz, 1, 1)
        for p in range(3):
            landed(p, at)
            send(p, at, twin)
    for dz in range(depth):
        for dy in range(2):
            for dx in range(2):
                for p in range(3):
                    landed(p, block(dz, dy, dx, 1))
    for copy in keep:
        copy.wait()
    for p in range(3):
        for copy in sent[p]:
            copy.wait_send()


def gather_all(table, tokens, cotangent):
    count = lax.axis_size("expert") * lax.axis_size("tensor")
    depth = lax.axis_size("expert") // 2
    parts = (table, tokens, cotangent)
    return pl.pallas_call(
        lambda *refs: gather_kernel(depth, *refs),
        out_shape=[jax.ShapeDtypeStruct((count, *a.shape), a.dtype) for a in parts],
        in_specs=[pl.BlockSpec(memory_space=pltpu.VMEM)] * 3,
        out_specs=[pl.BlockSpec(memory_space=pl.ANY)] * 3,
        scratch_shapes=[
            pltpu.SemaphoreType.DMA((3, count - 1)),
            pltpu.SemaphoreType.DMA((3, count)),
            pltpu.SemaphoreType.DMA((3,)),
        ],
        compiler_params=pltpu.CompilerParams(collective_id=0, has_side_effects=True),
    )(*parts)


def scatter_kernel(depth, part, out, total, twin_in, x_in, y_in, z_in, send_sem, recv_sem):
    z, y, x, c = place()
    along, over_y, over_x, twin = peers(depth)
    rows = out.shape[0] // 2
    halves = [pl.ds(0, rows), pl.ds(rows, rows)]
    sent = []

    def block(dz, dy, dx, dc=0):
        zz = lax.rem(z + dz, depth)
        yy, xx, cc = (1 - y if dy else y), (1 - x if dx else x), (1 - c if dc else c)
        return (zz * 2 + yy) * 4 + xx * 2 + cc

    def send(src, dst, device):
        copy = pltpu.make_async_remote_copy(
            src_ref=src,
            dst_ref=dst,
            send_sem=send_sem.at[len(sent)],
            recv_sem=recv_sem.at[len(sent)],
            device_id=device,
            device_id_type=MESH,
        )
        copy.start()
        sent.append(copy)
        return copy

    def add(a, b):
        return (a.astype(jnp.float32) + b.astype(jnp.float32)).astype(jnp.bfloat16)

    steps = [*range(1, depth), 0]
    corners = ((1, 1), (0, 1), (1, 0), (0, 0))
    greet(depth)
    from_twin, over, last, ends = {}, {}, {}, {}
    for dz in steps:
        for dy, dx in corners:
            i = dz * 4 + dy * 2 + dx
            from_twin[i] = send(part.at[block(dz, dy, dx, 1)], twin_in.at[i], twin)

    def merge(half, dz, other):
        over[half, dz, other].wait_recv()
        if half == 0:
            i, got = dz * 4 + other * 2, x_in.at[dz * 2 + other]
        else:
            i, got = dz * 4 + other, y_in.at[dz * 2 + other]
        total[i, halves[half]] = add(total[i, halves[half]], got[...])
        return i

    def first(dz):
        for dy, dx in corners:
            i = dz * 4 + dy * 2 + dx
            from_twin[i].wait_recv()
            total[i] = add(part[block(dz, dy, dx)], twin_in[i])
            if dx:
                over[0, dz, dy] = send(total.at[i, halves[0]], x_in.at[dz * 2 + dy], over_x)
            if dy:
                over[1, dz, dx] = send(total.at[i, halves[1]], y_in.at[dz * 2 + dx], over_y)

    def second(dz):
        i = merge(0, dz, 1)
        last[0, dz] = send(total.at[i, halves[0]], y_in.at[depth * 2 + dz], over_y)
        i = merge(1, dz, 1)
        last[1, dz] = send(total.at[i, halves[1]], x_in.at[depth * 2 + dz], over_x)

    def third(dz):
        for half in range(2):
            i = merge(half, dz, 0)
            last[half, dz].wait_recv()
            got = (x_in if half else y_in)[depth * 2 + dz]
            total[i, halves[half]] = add(total[i, halves[half]], got)
            if dz:
                ends[half, dz] = send(
                    total.at[i, halves[half]], z_in.at[half * (depth - 1) + dz - 1], along[dz - 1]
                )

    for turn in range(depth + 2):
        for stage, lag in ((first, 0), (second, 1), (third, 2)):
            if 0 <= turn - lag < depth:
                stage(steps[turn - lag])
    for half in range(2):
        value = total[0, halves[half]].astype(jnp.float32)
        for dz in range(1, depth):
            ends[half, dz].wait_recv()
            value = value + z_in[half * (depth - 1) + dz - 1].astype(jnp.float32)
        out[halves[half]] = value.astype(jnp.bfloat16)
    for copy in sent:
        copy.wait_send()


def scatter_sum(part, rows):
    width = part.shape[1]
    depth = lax.axis_size("expert") // 2
    copies = depth * 4 + 2 * (depth * 2 + depth + depth - 1)
    half = rows // 2
    return pl.pallas_call(
        lambda *refs: scatter_kernel(depth, *refs),
        out_shape=jax.ShapeDtypeStruct((rows, width), jnp.bfloat16),
        in_specs=[pl.BlockSpec(memory_space=pltpu.VMEM)],
        out_specs=pl.BlockSpec(memory_space=pltpu.VMEM),
        scratch_shapes=[
            pltpu.VMEM((depth * 4, rows, width), jnp.bfloat16),
            pltpu.VMEM((depth * 4, rows, width), jnp.bfloat16),
            pltpu.VMEM((depth * 3, half, width), jnp.bfloat16),
            pltpu.VMEM((depth * 3, half, width), jnp.bfloat16),
            pltpu.VMEM((depth * 2 - 2, half, width), jnp.bfloat16),
            pltpu.SemaphoreType.DMA((copies,)),
            pltpu.SemaphoreType.DMA((copies,)),
        ],
        compiler_params=pltpu.CompilerParams(
            collective_id=1, has_side_effects=True, vmem_limit_bytes=48 * 1024 * 1024
        ),
    )(part.reshape(-1, rows, width))


def dense(tokens, cotangent, routes, combine, w_gate, w_up, w_down):
    rows, width = tokens.shape
    experts = lax.axis_size("expert") * w_gate.shape[0]
    named = routes[:, :, None] == jnp.arange(experts, dtype=jnp.int32)[None, None, :]
    table = jnp.sum(jnp.where(named, combine[:, :, None], 0.0), axis=1).T
    table, xs, cot = gather_all(table, tokens, cotangent)
    xs = xs.reshape(-1, width)
    scale = lax.dynamic_slice_in_dim(table, lax.axis_index("expert"), 1, axis=1).reshape(-1, 1)
    dys = (scale * cot.reshape(-1, width).astype(jnp.float32)).astype(jnp.bfloat16)
    gate_w = w_gate[0]
    up_w = w_up[0]
    down_w = w_down[0]
    gate = jnp.dot(xs, gate_w, preferred_element_type=jnp.float32)
    upper = jnp.dot(xs, up_w, preferred_element_type=jnp.float32)
    sigma = jax.nn.sigmoid(gate)
    act = (gate * sigma * upper).astype(jnp.bfloat16)
    d_act = contract_cols(dys, down_w)
    d_upper = (d_act * gate * sigma).astype(jnp.bfloat16)
    d_gate = (d_act * upper * sigma * (1.0 + gate * (1.0 - sigma))).astype(jnp.bfloat16)
    part = contract_cols(d_gate, gate_w) + contract_cols(d_upper, up_w)
    token_grad = scatter_sum(part.astype(jnp.bfloat16), rows)
    down_grad = contract_rows(act, dys).astype(jnp.bfloat16)
    gate_grad = contract_rows(xs, d_gate).astype(jnp.bfloat16)
    up_grad = contract_rows(xs, d_upper).astype(jnp.bfloat16)
    return (token_grad, gate_grad[None], up_grad[None], down_grad[None])


def on_device(tokens, cotangent, routes, combine, w_gate, w_up, w_down):
    groups, shards = lax.axis_size("expert"), lax.axis_size("tensor")
    rows, top_count = routes.shape
    few = w_gate.shape[0] == 1 and groups <= 2 * top_count
    plan = dense if few and shards == 4 and groups % 2 == 0 and rows % 32 == 0 else slotted
    return plan(tokens, cotangent, routes, combine, w_gate, w_up, w_down)


def solution(mesh):
    in_specs = (
        P(("expert", "tensor"), None),
        P(("expert", "tensor"), None),
        P(("expert", "tensor"), None),
        P(("expert", "tensor"), None),
        P("expert", None, "tensor"),
        P("expert", None, "tensor"),
        P("expert", "tensor", None),
    )
    out_specs = (
        P(("expert", "tensor"), None),
        P("expert", None, "tensor"),
        P("expert", None, "tensor"),
        P("expert", "tensor", None),
    )
    return jax.shard_map(
        on_device, mesh=mesh, in_specs=in_specs, out_specs=out_specs, check_vma=False
    )
```

profile of v0, /device:TPU:0, one launch (start us, length us, event | category | flops | bytes accessed | tf_op | source)
XLA Modules:
  0.0 180.7 jit_solution(2472327034074490728)
XLA Ops:
  0.6 0.0 copy-start
  0.7 1.4 select_reduce_fusion
  2.1 68.4 %shard_map.102 = (f32[32,8,32]{2,1,0:T(8,128)}, bf16[32,32,2880]{2,1,0:T(8,128)(2,1)}, bf16[32,32,2880]{2,1,0:T(8,128)(2,1)}) custom-call(f32[8,32]{1,0:T(8,128)} %bitcast.45, bf16[32,2880]{1,0:T(8,128)(2,1)} %refs_1_.1, bf16[32,2880]{1,0:T(8,128)(2,1)} %refs_2_.1), custom_call_target="tpu_custom_call" | custom-call | tf_op jit(solution)/shard_map/pallas_call | solution.py:191
  70.5 0.5 broadcast.17
  71.0 1.6 fusion.15
  72.6 0.1 mul.52
  72.7 0.0 copy-done
  72.7 0.0 copy-start.2
  72.7 6.5 %fusion.6 = f32[1024,360]{0,1:T(8,128)} fusion(bf16[1024,2880]{1,0:T(8,128)(2,1)} %bitcast.46, bf16[1,2880,360]{1,2,0:T(8,128)(2,1)S(1)} %copy-done), kind=kOutput, calls=%fused_computation.12 | convolution fusion | flops 2123366400 | bytes 9446400 | tf_op jit(solution)/shard_map/dot_general | solution.py:329
  79.2 0.0 copy-done.2
  79.2 0.0 copy-done.3
  79.2 3.6 %fusion.9 = f32[1024,360]{0,1:T(8,128)} fusion(bf16[1024,2880]{1,0:T(8,128)(2,1)S(1)} %bitcast.48, bf16[1,2880,360]{1,2,0:T(8,128)(2,1)S(1)} %copy-done.2), kind=kOutput, calls=%fused_computation.15 | convolution fusion | flops 2123366400 | bytes 9446400 | tf_op jit(solution)/shard_map/dot_general | solution.py:330
  82.8 0.0 slice-done
  82.8 0.0 slice-done.1
  82.8 2.0 %multiply_convert_fusion = bf16[32,32,2880]{2,1,0:T(8,128)(2,1)S(1)} fusion(f32[32,32]{1,0:T(8,128)S(1)} %bitcast.44, bf16[32,32,2880]{2,1,0:T(8,128)(2,1)S(1)} %bitcast.42), kind=kLoop, calls=%fused_computation.2 | loop fusion | flops 8847360 | bytes 11800576 | tf_op jit(solution)/shard_map/convert_element_type | solution.py:325
  84.8 4.6 %fusion = bf16[1024,2880]{1,0:T(8,128)(2,1)} fusion(f32[1024]{0:T(1024)S(1)} %mul.52, bf16[32,32,2880]{2,1,0:T(8,128)(2,1)S(1)} %bitcast.42), kind=kLoop, calls=%fused_computation.1 | loop fusion | flops 8847360 | bytes 11800576 | tf_op jit(solution)/shard_map/convert_element_type | solution.py:325
  89.4 7.6 %fusion.3 = bf16[1,360,2880]{2,1,0:T(8,128)(2,1)} fusion(bf16[1024,2880]{1,0:T(8,128)(2,1)} %fusion, f32[1024,360]{0,1:T(8,128)} %fusion.9, f32[1024,360]{0,1:T(8,128)} %fusion.6), kind=kOutput, calls=%fused_computation.9 | convolution fusion | flops 2126615040 | bytes 10920960 | tf_op jit(solution)/shard_map/dot_general | solution.py:19
  97.0 0.0 copy-done.4
  97.0 0.0 copy-done.5
  97.0 0.0 copy-done.6
  97.0 0.0 slice-start.3
  97.0 3.1 %multiply_convert_fusion.2 = (bf16[1024,360]{0,1:T(8,128)(2,1)S(1)}, bf16[1024,360]{0,1:T(8,128)(2,1)S(1)}) fusion(f32[1024,360]{0,1:T(8,128)S(1)} %copy-done.5, f32[1024,360]{0,1:T(8,128)S(1)} %copy-done.6, bf16[1024,2880]{1,0:T(8,128)(2,1)S(1)} %bitcast.43, bf16[1,360,2880]{2,1,0:T(8,128)(2,1)S(1)} %copy-done.4), kind=kOutput, calls=%fused_computation.20 | convolution fusion | flops 2128158720 | bytes 12395520 | tf_op jit(solution)/shard_map/dot_general | solution.py:25
  100.1 6.5 %fusion.2 = bf16[1,2880,360]{1,2,0:T(8,128)(2,1)} fusion(bf16[1024,2880]{1,0:T(8,128)(2,1)} %bitcast.47, bf16[1024,360]{0,1:T(8,128)(2,1)S(1)} %get-tuple-element.12), kind=kOutput, calls=%fused_computation.8 | convolution fusion | flops 2124403200 | bytes 8709120 | tf_op jit(solution)/shard_map/dot_general | solution.py:19
  106.6 0.0 slice-done.2
  106.6 0.0 slice-done.3
  106.6 3.9 %fusion.1 = bf16[1,2880,360]{1,2,0:T(8,128)(2,1)} fusion(bf16[1024,2880]{1,0:T(8,128)(2,1)S(1)} %bitcast.51, bf16[1024,360]{0,1:T(8,128)(2,1)S(1)} %get-tuple-element.13), kind=kOutput, calls=%fused_computation.7 | convolution fusion | flops 2124403200 | bytes 8709120 | tf_op jit(solution)/shard_map/dot_general | solution.py:19
  110.4 3.3 %fusion.4 = f32[1024,2880]{0,1:T(8,128)S(1)} fusion(bf16[1024,360]{0,1:T(8,128)(2,1)S(1)} %get-tuple-element.13, bf16[1,2880,360]{1,2,0:T(8,128)(2,1)S(1)} %copy-done), kind=kOutput, calls=%fused_computation.10 | convolution fusion | flops 2123366400 | bytes 14607360 | tf_op jit(solution)/shard_map/dot_general | solution.py:25
  113.8 5.3 %add_convert_fusion = bf16[1024,2880]{0,1:T(8,128)(2,1)} fusion(f32[1024,2880]{0,1:T(8,128)S(1)} %fusion.4, bf16[1024,360]{0,1:T(8,128)(2,1)S(1)} %get-tuple-element.12, bf16[1,2880,360]{1,2,0:T(8,128)(2,1)S(1)} %copy-done.2), kind=kOutput, calls=%fused_computation.3 | convolution fusion | flops 2129264640 | bytes 20505600 | tf_op jit(solution)/shard_map/dot_general | solution.py:25
  119.1 8.5 %copy.14 = bf16[1024,2880]{1,0:T(8,128)(2,1)} copy(bf16[1024,2880]{0,1:T(8,128)(2,1)} %add_convert_fusion) | data formatting | bytes 11796480 | tf_op jit(solution)/shard_map/convert_element_type | solution.py:337
  127.6 2.7 %copy-done.1 = bf16[1024,2880]{1,0:T(8,128)(2,1)S(1)} copy-done((bf16[1024,2880]{1,0:T(8,128)(2,1)S(1)}, bf16[1024,2880]{1,0:T(8,128)(2,1)}, u32[]{:S(2)}) %copy-start.1) | copy-done | bytes 5898264
  130.3 49.6 %shard_map.103 = bf16[32,2880]{1,0:T(8,128)(2,1)S(1)} custom-call(bf16[32,32,2880]{2,1,0:T(8,128)(2,1)S(1)} %bitcast.40), custom_call_target="tpu_custom_call" | custom-call | tf_op jit(solution)/shard_map/pallas_call | solution.py:297
  180.0 0.7 copy.16
  (10 shorter events, 0.0 us)
Async XLA Ops:
  0.6 72.1 %copy-start = (bf16[1,2880,360]{1,2,0:T(8,128)(2,1)S(1)}, bf16[1,2880,360]{1,2,0:T(8,128)(2,1)}, u32[]{:S(2)}) copy-start(bf16[1,2880,360]{1,2,0:T(8,128)(2,1)} %param.11) | copy-start | bytes 6220804
  72.7 6.5 %copy-start.2 = (bf16[1,2880,360]{1,2,0:T(8,128)(2,1)S(1)}, bf16[1,2880,360]{1,2,0:T(8,128)(2,1)}, u32[]{:S(2)}) copy-start(bf16[1,2880,360]{1,2,0:T(8,128)(2,1)} %param.12) | copy-start | bytes 6220804
  72.7 6.5 %copy-start.3 = (bf16[32,32,2880]{2,1,0:T(8,128)(2,1)S(1)}, bf16[32,32,2880]{2,1,0:T(8,128)(2,1)}, u32[]{:S(2)}) copy-start(bf16[32,32,2880]{2,1,0:T(8,128)(2,1)} %get-tuple-element.9) | copy-start | bytes 17694724
  72.7 10.1 %slice-start = ((s8[6029312]{0:T(1024)(128)(4,1)}), s8[4194304]{0:T(1024)(128)(4,1)S(1)}, s32[]{:S(2)}) async-start(s8[6029312]{0:T(1024)(128)(4,1)} %bitcast.41), calls=%async_computation | async-start | bytes 8388608
  79.2 3.6 %slice-start.1 = ((s8[6029312]{0:T(1024)(128)(4,1)}), s8[1835008]{0:T(1024)(128)(4,1)S(1)}, s32[]{:S(2)}) async-start(s8[6029312]{0:T(1024)(128)(4,1)} %bitcast.41), calls=%async_computation.1 | async-start | bytes 3670016
  89.4 7.6 %copy-start.4 = (bf16[1,360,2880]{2,1,0:T(8,128)(2,1)S(1)}, bf16[1,360,2880]{2,1,0:T(8,128)(2,1)}, u32[]{:S(2)}) copy-start(bf16[1,360,2880]{2,1,0:T(8,128)(2,1)} %param.13) | copy-start | bytes 6220804
  89.4 7.6 %copy-start.5 = (f32[1024,360]{0,1:T(8,128)S(1)}, f32[1024,360]{0,1:T(8,128)}, u32[]{:S(2)}) copy-start(f32[1024,360]{0,1:T(8,128)} %fusion.6) | copy-start | bytes 4423684
  89.4 7.6 %copy-start.6 = (f32[1024,360]{0,1:T(8,128)S(1)}, f32[1024,360]{0,1:T(8,128)}, u32[]{:S(2)}) copy-start(f32[1024,360]{0,1:T(8,128)} %fusion.9) | copy-start | bytes 4423684
  89.4 17.2 %slice-start.2 = ((s8[6029312]{0:T(1024)(128)(4,1)}), s8[4194304]{0:T(1024)(128)(4,1)S(1)}, s32[]{:S(2)}) async-start(s8[6029312]{0:T(1024)(128)(4,1)} %bitcast.49), calls=%async_computation.2 | async-start | bytes 8388608
  97.0 9.6 %slice-start.3 = ((s8[6029312]{0:T(1024)(128)(4,1)}), s8[1835008]{0:T(1024)(128)(4,1)S(1)}, s32[]{:S(2)}) async-start(s8[6029312]{0:T(1024)(128)(4,1)} %bitcast.49), calls=%async_computation.3 | async-start | bytes 3670016
  127.6 2.7 %copy-start.1 = (bf16[1024,2880]{1,0:T(8,128)(2,1)S(1)}, bf16[1024,2880]{1,0:T(8,128)(2,1)}, u32[]{:S(2)}) copy-start(bf16[1024,2880]{1,0:T(8,128)(2,1)} %copy.14) | copy-start | bytes 17694724
where the time goes:
time: 181 us
  Pallas kernels  118 us (65%)
  matrix products  39.8 us (22%)
  local copies, waits for them, and re-layouts  14.1 us (8%)
  other arithmetic  8.02 us (4%)
    pallas_call x1, Pallas kernels, gather_all(): pl.pallas_call(lambda *refs: gather_kernel(depth, *refs), out_shape=[jax....  68.4 us
    pallas_call x1, Pallas kernels, scatter_sum(): pl.pallas_call(lambda *refs: scatter_kernel(depth, *refs), out_shape=jax....  49.6 us
    dot_general x3, matrix products, contract_rows(): lax.dot_general(left, right, (((0,), (0,)), ((), ())), preferred_element_...  17.9 us
    dot_general x3, matrix products, contract_cols(): lax.dot_general(left, right, (((1,), (1,)), ((), ())), preferred_element_...  11.7 us
    convert_element_type x1, local copies, waits for them, and re-layouts, dense(): token_grad = scatter_sum(part.astype(jnp.bfloat16), rows)  8.52 us
    convert_element_type x2, other arithmetic, dense(): (scale * cot.reshape(-1, width).astype(jnp.float32)).astype(jnp.bfloat16)  6.57 us
    dot_general x1, matrix products, dense(): gate = jnp.dot(xs, gate_w, preferred_element_type=jnp.float32)  6.46 us
    dot_general x1, matrix products, dense(): upper = jnp.dot(xs, up_w, preferred_element_type=jnp.float32)  3.64 us

commit v1 on v0

--- a/solution.py
+++ b/solution.py
@@ -341,11 +341,461 @@
     return (token_grad, gate_grad[None], up_grad[None], down_grad[None])
 
 
+def line_order(depth, z):
+    others = sorted((abs(p - z), p) for p in range(depth) if p != z)
+    return [z] + [p for _, p in others]
+
+
+def pad_to(value, unit):
+    return -(-value // unit) * unit
+
+
+def tiles(total, size):
+    full = total // size
+    return full, total - full * size
+
+
+def contract_first(left, right):
+    return lax.dot_general(
+        left, right, (((0,), (0,)), ((), ())), preferred_element_type=jnp.float32
+    )
+
+
+def fused_kernel(depth, experts, tok, cot, routes, comb, w_gate, w_up, w_down,
+                 tg, gg, ug, dg,
+                 xs, ct, dys, part, wide, g_raw, u_raw, d_raw, dgu, act_t, d_act, scl,
+                 gg_buf, ug_buf, dg_buf, twin_in, total, x_in, y_in, z_in,
+                 g_send, g_recv, s_send, s_recv, w_sem, o_sem):
+    rows, width = tok.shape
+    hid = d_raw.shape[0]
+    wpad = xs.shape[1]
+    hpad = d_act.shape[1]
+    blocks = hpad // 128
+    chunk = rows * 8
+    z, y, x, c = place()
+    t = x * 2 + c
+    along, over_y, over_x, twin = peers(depth)
+    above, below = (z * 2 + 2 + y, t), (z * 2 - 2 + y, t)
+    table = [line_order(depth, zz) for zz in range(depth)]
+
+    def plane(i):
+        if i == 0:
+            return z
+        value = 0
+        for zz in range(depth):
+            value = value + jnp.where(z == zz, table[zz][i], 0)
+        return value
+
+    planes = [plane(i) for i in range(depth)]
+
+    def block(p, dy, dx, dc=0):
+        yy, xx, cc = (1 - y if dy else y), (1 - x if dx else x), (1 - c if dc else c)
+        return (p * 2 + yy) * 4 + xx * 2 + cc
+
+    def at_rows(at, count=rows):
+        return pl.ds(pl.multiple_of(at * rows, rows), count)
+
+    bufs = (xs, ct)
+    sent = []
+    counts = [0, 0]
+
+    loads = [
+        pltpu.make_async_copy(w_gate.at[0], g_raw, w_sem.at[0]),
+        pltpu.make_async_copy(w_up.at[0], u_raw, w_sem.at[1]),
+        pltpu.make_async_copy(w_down.at[0], d_raw, w_sem.at[2]),
+    ]
+    for load in loads:
+        load.start()
+
+    me = block(z, 0, 0)
+    lane = lax.broadcasted_iota(jnp.int32, (rows, 128), 1)
+    first_lane = width - (wpad - 128)
+    owner = lax.rem(lane - first_lane + experts, experts)
+    named = jnp.zeros((rows, 128), jnp.float32)
+    for k in range(routes.shape[1]):
+        named = named + jnp.where(routes[:, k : k + 1] == owner, comb[:, k : k + 1], 0.0)
+    high = named.astype(jnp.bfloat16).astype(jnp.float32)
+    mid = (named - high).astype(jnp.bfloat16).astype(jnp.float32)
+    low = named - high - mid
+    piece = jnp.where(lane < first_lane + experts, high, jnp.where(lane < first_lane + 2 * experts, mid, low))
+    piece = jnp.where(lane < first_lane + 3 * experts, piece, 0.0)
+    tail = jnp.concatenate(
+        [tok[:, wpad - 128 : width].astype(jnp.float32), jnp.zeros((rows, wpad - width), jnp.float32)], axis=1
+    )
+    xs[at_rows(me), : wpad - 128] = tok[:, : wpad - 128]
+    xs[at_rows(me), wpad - 128 :] = jnp.where(lane < first_lane, tail, piece).astype(jnp.bfloat16)
+    ct[at_rows(me), :] = cot[...]
+    greet(depth)
+
+    def send(q, at, device, cond=None):
+        copy = pltpu.make_async_remote_copy(
+            src_ref=bufs[q].at[at_rows(at)],
+            dst_ref=bufs[q].at[at_rows(at)],
+            send_sem=g_send.at[q, counts[q]],
+            recv_sem=g_recv.at[q, at],
+            device_id=device,
+            device_id_type=MESH,
+        )
+        counts[q] += 1
+        if cond is None:
+            copy.start()
+        else:
+            pl.when(cond)(copy.start)
+        sent.append((copy, cond))
+
+    def landed(q, at):
+        pltpu.make_async_remote_copy(
+            src_ref=bufs[q].at[at_rows(at)],
+            dst_ref=bufs[q].at[at_rows(at)],
+            send_sem=g_send.at[q, 0],
+            recv_sem=g_recv.at[q, at],
+            device_id=twin,
+            device_id_type=MESH,
+        ).wait_recv()
+
+    def send_z(q, i, at):
+        if i == 0:
+            send(q, at, above, z < depth - 1)
+            send(q, at, below, z > 0)
+        else:
+            up = planes[i] < z
+            zz = jnp.where(up, z + 1, z - 1)
+            onward = jnp.where(up, z < depth - 1, z > 0)
+            send(q, at, (zz * 2 + y, t), onward)
+
+    def first(i):
+        at = block(planes[i], 0, 0)
+        for q in range(2):
+            if i:
+                landed(q, at)
+            send_z(q, i, at)
+            send(q, at, over_x)
+            send(q, at, over_y)
+            send(q, at, twin)
+
+    def second(i):
+        by_y, by_x = block(planes[i], 1, 0), block(planes[i], 0, 1)
+        for q in range(2):
+            near, far, onward = (by_x, by_y, over_y) if q else (by_y, by_x, over_x)
+            landed(q, near)
+            if i == 0 or q not in ZDIAG:
+                send(q, near, onward)
+            send(q, near, twin)
+            landed(q, far)
+            send(q, far, twin)
+
+    def third(i):
+        at = block(planes[i], 1, 1)
+        for q in range(2):
+            landed(q, at)
+            if q in ZDIAG:
+                send_z(q, i, at)
+            send(q, at, twin)
+
+    def fourth(i):
+        for dy in range(2):
+            for dx in range(2):
+                for q in range(2):
+                    landed(q, block(planes[i], dy, dx, 1))
+
+    def prepare():
+        for load in loads:
+            load.wait()
+        wide[width:, :] = jnp.zeros((wpad - width, wide.shape[1]), jnp.bfloat16)
+        for raw, side in ((g_raw, 0), (u_raw, 1)):
+            for j in range(blocks):
+                to = 256 * j + 128 * side
+                live = min(128, hid - 128 * j)
+                if live < 128:
+                    wide[:width, to : to + 128] = jnp.zeros((width, 128), jnp.bfloat16)
+                wide[:width, to : to + live] = raw[:, 128 * j : 128 * j + live]
+        d_act[...] = jnp.zeros(d_act.shape, jnp.float32)
+
+    def compute(i):
+        r0 = pl.multiple_of(planes[i] * chunk, chunk)
+        here = pl.ds(r0, chunk)
+        spot = lax.broadcasted_iota(jnp.int32, (chunk, 128), 1) - first_lane
+        e = lax.axis_index("expert")
+        mine = (spot == e) | (spot == e + experts) | (spot == e + 2 * experts)
+        scale = jnp.sum(jnp.where(mine, xs[here, wpad - 128 :].astype(jnp.float32), 0.0), axis=1, keepdims=True)
+        scl[...] = jnp.broadcast_to(scale, (chunk, 128))
+
+        def scaled(k, _):
+            at = pl.ds(pl.multiple_of(r0 + k * 16, 16), 16)
+            by = scl[pl.ds(pl.multiple_of(k * 16, 16), 16), 0:1]
+            dys[at, :] = (by * ct[at, :].astype(jnp.float32)).astype(jnp.bfloat16)
+            return 0
+
+        lax.fori_loop(0, chunk // 16, scaled, 0)
+        d_act[:, :hid] = contract_cols(dys[here, :], d_raw[...])
+
+        def gates(j, _):
+            cols = pl.ds(pl.multiple_of(j * 256, 256), 256)
+            both = jnp.dot(xs[here, :], wide[:, cols], preferred_element_type=jnp.float32)
+            gate, upper = both[:, :128], both[:, 128:]
+            da = d_act[:, pl.ds(pl.multiple_of(j * 128, 128), 128)]
+            sigma = jax.nn.sigmoid(gate)
+            act = gate * sigma * upper
+            act_t[pl.ds(pl.multiple_of(j * 128, 128), 128), here] = act.T.astype(jnp.bfloat16)
+            dgu[here, pl.ds(pl.multiple_of(j * 256, 256), 128)] = (
+                da * upper * sigma * (1.0 + gate * (1.0 - sigma))
+            ).astype(jnp.bfloat16)
+            dgu[here, pl.ds(pl.multiple_of(j * 256 + 128, 128), 128)] = (da * gate * sigma).astype(jnp.bfloat16)
+            return 0
+
+        lax.fori_loop(0, blocks, gates, 0)
+        size = 512
+        full, rest = tiles(width, size)
+
+        def back(k, _):
+            cols = pl.ds(pl.multiple_of(k * size, size), size)
+            part[here, cols] = contract_cols(dgu[here, :], wide[cols, :]).astype(jnp.bfloat16)
+            return 0
+
+        lax.fori_loop(0, full, back, 0)
+        if rest:
+            part[here, full * size : width] = contract_cols(
+                dgu[here, :], wide[full * size : width, :]
+            ).astype(jnp.bfloat16)
+
+    half = rows // 2
+    halves = [pl.ds(0, half), pl.ds(half, half)]
+    ssent = []
+
+    def ssend(src, dst, device, recv):
+        copy = pltpu.make_async_remote_copy(
+            src_ref=src,
+            dst_ref=dst,
+            send_sem=s_send.at[len(ssent)],
+            recv_sem=s_recv.at[recv] if recv is not None else s_recv.at[len(ssent)],
+            device_id=device,
+            device_id_type=MESH,
+        )
+        copy.start()
+        ssent.append(copy)
+        return copy
+
+    def add(a, b):
+        return (a.astype(jnp.float32) + b.astype(jnp.float32)).astype(jnp.bfloat16)
+
+    corners = ((1, 1), (0, 1), (1, 0), (0, 0))
+    from_twin, over, last = {}, {}, {}
+    z_base = depth * 10
+
+    def s0(i):
+        for dy, dx in corners:
+            k = i * 4 + dy * 2 + dx
+            from_twin[k] = ssend(part.at[at_rows(block(planes[i], dy, dx, 1))], twin_in.at[k], twin, k)
+
+    def merge(h, i, other):
+        over[h, i, other].wait_recv()
+        if h == 0:
+            k, got = i * 4 + other * 2, x_in.at[i * 2 + other]
+        else:
+            k, got = i * 4 + other, y_in.at[i * 2 + other]
+        total[k, halves[h]] = add(total[k, halves[h]], got[...])
+        return k
+
+    def s1(i):
+        for dy, dx in corners:
+            k = i * 4 + dy * 2 + dx
+            from_twin[k].wait_recv()
+            total[k] = add(part[at_rows(block(planes[i], dy, dx)), :], twin_in[k])
+            if dx:
+                over[0, i, dy] = ssend(total.at[k, halves[0]], x_in.at[i * 2 + dy], over_x, depth * 4 + i * 2 + dy)
+            if dy:
+                over[1, i, dx] = ssend(total.at[k, halves[1]], y_in.at[i * 2 + dx], over_y, depth * 6 + i * 2 + dx)
+
+    def s2(i):
+        k = merge(0, i, 1)
+        last[0, i] = ssend(total.at[k, halves[0]], y_in.at[depth * 2 + i], over_y, depth * 8 + i)
+        k = merge(1, i, 1)
+        last[1, i] = ssend(total.at[k, halves[1]], x_in.at[depth * 2 + i], over_x, depth * 9 + i)
+
+    def s3(i):
+        for h in range(2):
+            k = merge(h, i, 0)
+            last[h, i].wait_recv()
+            got = (x_in if h else y_in)[depth * 2 + i]
+            total[k, halves[h]] = add(total[k, halves[h]], got)
+            if i:
+                ssend(
+                    total.at[k, halves[h]], z_in.at[h * depth + z], (planes[i] * 2 + y, t), z_base + h * depth + z
+                )
+
+    def finish():
+        for h in range(2):
+            value = total[0, halves[h]].astype(jnp.float32)
+            for step in range(1, depth):
+                zz = lax.rem(z + step, depth)
+                at = h * depth + zz
+                pltpu.make_async_remote_copy(
+                    src_ref=total.at[0, halves[h]],
+                    dst_ref=z_in.at[at],
+                    send_sem=s_send.at[0],
+                    recv_sem=s_recv.at[z_base + at],
+                    device_id=twin,
+                    device_id_type=MESH,
+                ).wait_recv()
+                value = value + z_in[at].astype(jnp.float32)
+            tg[halves[h], :] = value.astype(jnp.bfloat16)
+
+    msize = 384
+    mfull, mrest = tiles(wpad, msize)
+
+    def wide_tile(start, size, valid):
+        out = contract_first(xs[:, pl.ds(start, size)], dgu[...])
+        for j in range(blocks):
+            live = min(128, hid - 128 * j)
+            for buf, side in ((gg_buf, 0), (ug_buf, 1)):
+                at = 256 * j + 128 * side
+                buf[pl.ds(start, valid), 128 * j : 128 * j + live] = out[:valid, at : at + live].astype(jnp.bfloat16)
+
+    def wide_grads(lo, hi):
+        def body(k, _):
+            wide_tile(pl.multiple_of(k * msize, msize), msize, msize)
+            return 0
+
+        lax.fori_loop(lo, hi, body, 0)
+
+    def wide_rest():
+        if mrest:
+            wide_tile(mfull * msize, mrest, width - mfull * msize)
+        for q, (src, dst) in enumerate(((gg_buf, gg), (ug_buf, ug))):
+            outs.append(pltpu.make_async_copy(src, dst.at[0], o_sem.at[q]))
+            outs[-1].start()
+
+    nsize = 512
+    nfull, nrest = tiles(width, nsize)
+    outs = []
+
+    def down_grads():
+        def body(k, _):
+            cols = pl.ds(pl.multiple_of(k * nsize, nsize), nsize)
+            dg_buf[:, cols] = jnp.dot(
+                act_t[...], dys[:, cols], preferred_element_type=jnp.float32
+            )[:hid].astype(jnp.bfloat16)
+            return 0
+
+        lax.fori_loop(0, nfull, body, 0)
+        if nrest:
+            dg_buf[:, nfull * nsize : width] = jnp.dot(
+                act_t[...], dys[:, nfull * nsize : width], preferred_element_type=jnp.float32
+            )[:hid].astype(jnp.bfloat16)
+        outs.append(pltpu.make_async_copy(dg_buf, dg.at[0], o_sem.at[2]))
+        outs[-1].start()
+
+    first(0)
+    prepare()
+    for i in range(depth):
+        if i == 0 and depth > 1:
+            first(1)
+            second(0)
+        if i == 0 and depth == 1:
+            second(0)
+        third(i)
+        if i + 2 < depth:
+            first(i + 2)
+        if i + 1 < depth:
+            second(i + 1)
+        for lag, stage in ((1, s1), (2, s2), (3, s3)):
+            if i >= lag:
+                stage(i - lag)
+        fourth(i)
+        compute(i)
+        s0(i)
+    if depth > 1:
+        s2(depth - 2)
+    if depth > 2:
+        s3(depth - 3)
+    s1(depth - 1)
+    down_grads()
+    if depth > 1:
+        s3(depth - 2)
+    s2(depth - 1)
+    wide_grads(0, mfull // 2)
+    s3(depth - 1)
+    wide_grads(mfull // 2, mfull)
+    wide_rest()
+    finish()
+    for copy, cond in sent:
+        if cond is None:
+            copy.wait_send()
+        else:
+            pl.when(cond)(copy.wait_send)
+    for copy in ssent:
+        copy.wait_send()
+    for copy in outs:
+        copy.wait()
+
+
+ZDIAG = (0, 1)
+
+
+def fused(tokens, cotangent, routes, combine, w_gate, w_up, w_down):
+    rows, width = tokens.shape
+    hid = w_gate.shape[2]
+    groups = lax.axis_size("expert")
+    depth = groups // 2
+    wpad, hpad = pad_to(width, 128), pad_to(hid, 128)
+    count = groups * 4
+    everyone = count * rows
+    half = rows // 2
+    copies = depth * 4 + depth * 4 + depth * 2 + 2 * (depth - 1)
+    vmem = pl.BlockSpec(memory_space=pltpu.VMEM)
+    hbm = pl.BlockSpec(memory_space=pl.ANY)
+    bf16, f32 = jnp.bfloat16, jnp.float32
+    return pl.pallas_call(
+        lambda *refs: fused_kernel(depth, groups, *refs),
+        out_shape=[
+            jax.ShapeDtypeStruct(tokens.shape, bf16),
+            jax.ShapeDtypeStruct(w_gate.shape, bf16),
+            jax.ShapeDtypeStruct(w_up.shape, bf16),
+            jax.ShapeDtypeStruct(w_down.shape, bf16),
+        ],
+        in_specs=[vmem] * 4 + [hbm] * 3,
+        out_specs=[vmem] + [hbm] * 3,
+        scratch_shapes=[
+            pltpu.VMEM((everyone, wpad), bf16),
+            pltpu.VMEM((everyone, width), bf16),
+            pltpu.VMEM((everyone, width), bf16),
+            pltpu.VMEM((everyone, width), bf16),
+            pltpu.VMEM((wpad, 2 * hpad), bf16),
+            pltpu.VMEM((width, hid), bf16),
+            pltpu.VMEM((width, hid), bf16),
+            pltpu.VMEM((hid, width), bf16),
+            pltpu.VMEM((everyone, 2 * hpad), bf16),
+            pltpu.VMEM((hpad, everyone), bf16),
+            pltpu.VMEM((rows * 8, hpad), f32),
+            pltpu.VMEM((rows * 8, 128), f32),
+            pltpu.VMEM((width, hid), bf16),
+            pltpu.VMEM((width, hid), bf16),
+            pltpu.VMEM((hid, width), bf16),
+            pltpu.VMEM((depth * 4, rows, width), bf16),
+            pltpu.VMEM((depth * 4, rows, width), bf16),
+            pltpu.VMEM((depth * 3, half, width), bf16),
+            pltpu.VMEM((depth * 3, half, width), bf16),
+            pltpu.VMEM((depth * 2, half, width), bf16),
+            pltpu.SemaphoreType.DMA((2, depth * 9 + 2)),
+            pltpu.SemaphoreType.DMA((2, count)),
+            pltpu.SemaphoreType.DMA((copies,)),
+            pltpu.SemaphoreType.DMA((depth * 12,)),
+            pltpu.SemaphoreType.DMA((3,)),
+            pltpu.SemaphoreType.DMA((3,)),
+        ],
+        compiler_params=pltpu.CompilerParams(
+            collective_id=0, has_side_effects=True, vmem_limit_bytes=67_043_328
+        ),
+    )(tokens, cotangent, routes, combine, w_gate, w_up, w_down)
+
+
 def on_device(tokens, cotangent, routes, combine, w_gate, w_up, w_down):
     groups, shards = lax.axis_size("expert"), lax.axis_size("tensor")
     rows, top_count = routes.shape
     few = w_gate.shape[0] == 1 and groups <= 2 * top_count
-    plan = dense if few and shards == 4 and groups % 2 == 0 and rows % 32 == 0 else slotted
+    plan = slotted
+    if few and shards == 4 and groups % 2 == 0 and rows % 32 == 0:
+        plan = fused if -tokens.shape[1] % 128 >= 3 * groups else dense
     return plan(tokens, cotangent, routes, combine, w_gate, w_up, w_down)
 
 

time: 181 us -> 121 us (0.67)
  matrix products: 39.8 us -> 0 us
  Pallas kernels: 118 us -> 100 us
  other arithmetic: 8.02 us -> 0 us
  local copies, waits for them, and re-layouts: 14.1 us -> 20.1 us
    dot_general x8 -> x0, matrix products: 39.8 us -> none  [the longest x3 17.9 us: contract_rows(): lax.dot_general(left, right, (((0,), (0,)), ((), ())), preferred_element_...]
    pallas_call x2 -> x1, Pallas kernels: 118 us -> 100 us  [fused(): pl.pallas_call(lambda *refs: fused_kernel(depth, groups, *refs), out_shap...]
    unnamed x23 -> x12, local copies, waits for them, and re-layouts: 3.43 us -> 13.3 us
    convert_element_type x1 -> x0, local copies, waits for them, and re-layouts: 8.52 us -> none  [dense(): token_grad = scatter_sum(part.astype(jnp.bfloat16), rows)]
    pallas_call x0 -> x2, local copies, waits for them, and re-layouts: none -> 6.74 us  [fused(): pl.pallas_call(lambda *refs: fused_kernel(depth, groups, *refs), out_shap...]
    convert_element_type x2 -> x0, other arithmetic: 6.57 us -> none  [dense(): (scale * cot.reshape(-1, width).astype(jnp.float32)).astype(jnp.bfloat16)]
    dynamic_slice x2 -> x0, local copies, waits for them, and re-layouts: 2.12 us -> none  [dense(): lax.dynamic_slice_in_dim(table, lax.axis_index('expert'), 1, axis=1)]
where the time goes in v1:
time: 121 us
  Pallas kernels  100 us (83%)
  local copies, waits for them, and re-layouts  20.1 us (17%)
    pallas_call x1, Pallas kernels, fused(): pl.pallas_call(lambda *refs: fused_kernel(depth, groups, *refs), out_shap...  100 us
    unnamed x12, local copies, waits for them, and re-layouts  13.3 us
    pallas_call x2, local copies, waits for them, and re-layouts, fused(): pl.pallas_call(lambda *refs: fused_kernel(depth, groups, *refs), out_shap...  6.74 us

profile of v1, /device:TPU:0, one launch (start us, length us, event | category | flops | bytes accessed | tf_op | source)
XLA Modules:
  0.0 120.7 jit_solution(5536501455511504209)
XLA Ops:
  0.6 1.4 %copy.11.refs_2_ = s32[32,4]{1,0:T(8,128)} copy(s32[32,4]{0,1:T(4,128)} %param.9) | data formatting | bytes 1024 | tf_op args[2]
  2.0 1.4 %copy.12.refs_3_ = f32[32,4]{1,0:T(8,128)} copy(f32[32,4]{0,1:T(4,128)} %param.10) | data formatting | bytes 1024 | tf_op args[3]
  3.4 0.0 copy-start.1
  3.4 4.2 %copy.13.refs_4_ = bf16[1,2880,360]{2,1,0:T(8,128)(2,1)} copy(bf16[1,2880,360]{1,2,0:T(8,128)(2,1)} %param.11) | data formatting | bytes 4147200 | tf_op args[4]
  7.6 0.0 copy-done.1
  7.6 2.6 %copy.14.refs_5_ = bf16[1,2880,360]{2,1,0:T(8,128)(2,1)} copy(bf16[1,2880,360]{1,2,0:T(8,128)(2,1)S(1)} %copy-done.1) | data formatting | bytes 4147200 | tf_op args[5]
  10.2 100.0 %shard_map.102 = (bf16[32,2880]{1,0:T(8,128)(2,1)}, bf16[1,2880,360]{2,1,0:T(8,128)(2,1)}, bf16[1,2880,360]{2,1,0:T(8,128)(2,1)}, bf16[1,360,2880]{2,1,0:T(8,128)(2,1)}) custom-call(bf16[32,2880]{1,0:T(8,128)(2,1)} %refs_0_.1, bf16[32,2880]{1,0:T(8,128)(2,1)} %refs_1_.1, s32[32,4]{1,0:T(8,128)} %copy.11.refs_2_, f32[32,4]{1,0:T(8,128)} %copy.12.refs_3_, ...), custom_call_target="tpu_custom_call" | custom-call | tf_op jit(solution)/shard_map/pallas_call | solution.py:748
  110.2 0.0 copy-start
  110.2 4.3 %copy.15 = bf16[1,2880,360]{1,2,0:T(8,128)(2,1)} copy(bf16[1,2880,360]{2,1,0:T(8,128)(2,1)} %get-tuple-element.5) | data formatting | bytes 4147200 | tf_op jit(solution)/shard_map/pallas_call | solution.py:748
  114.5 0.0 copy-done
  114.5 0.0 copy-start.2
  114.5 2.5 %copy.16 = bf16[1,2880,360]{1,2,0:T(8,128)(2,1)} copy(bf16[1,2880,360]{2,1,0:T(8,128)(2,1)S(1)} %copy-done) | data formatting | bytes 4147200 | tf_op jit(solution)/shard_map/pallas_call | solution.py:748
  117.0 0.0 copy-done.2
  117.0 0.7 copy.19
  117.7 3.1 %copy.20 = bf16[1,360,2880]{2,1,0:T(8,128)(2,1)} copy(bf16[1,360,2880]{2,1,0:T(8,128)(2,1)} %get-tuple-element.15) | data formatting | bytes 4147200
Async XLA Ops:
  3.4 4.2 %copy-start.1 = (bf16[1,2880,360]{1,2,0:T(8,128)(2,1)S(1)}, bf16[1,2880,360]{1,2,0:T(8,128)(2,1)}, u32[]{:S(2)}) copy-start(bf16[1,2880,360]{1,2,0:T(8,128)(2,1)} %param.12) | copy-start | bytes 6220804
  110.2 4.3 %copy-start = (bf16[1,2880,360]{2,1,0:T(8,128)(2,1)S(1)}, bf16[1,2880,360]{2,1,0:T(8,128)(2,1)}, u32[]{:S(2)}) copy-start(bf16[1,2880,360]{2,1,0:T(8,128)(2,1)} %get-tuple-element.6) | copy-start | bytes 6220804
  114.5 2.5 %copy-start.2 = (bf16[32,2880]{1,0:T(8,128)(2,1)S(1)}, bf16[32,2880]{1,0:T(8,128)(2,1)}, u32[]{:S(2)}) copy-start(bf16[32,2880]{1,0:T(8,128)(2,1)} %get-tuple-element.12) | copy-start | bytes 552964

commit v2 on v0

--- a/solution.py
+++ b/solution.py
@@ -1,3 +1,5 @@
+import functools
+
 import jax
 import jax.numpy as jnp
 from jax import lax
@@ -341,11 +343,578 @@
     return (token_grad, gate_grad[None], up_grad[None], down_grad[None])
 
 
+def line_order(depth, z):
+    def key(p):
+        return abs(p - z), -abs(2 * p - depth + 1)
+
+    return sorted(range(depth), key=key)
+
+
+def pad_to(value, unit):
+    return -(-value // unit) * unit
+
+
+def tiles(total, size):
+    full = total // size
+    return full, total - full * size
+
+
+def contract_first(left, right):
+    return lax.dot_general(
+        left, right, (((0,), (0,)), ((), ())), preferred_element_type=jnp.float32
+    )
+
+
+def fused_kernel(depth, experts, tok, cot, routes, comb, w_gate, w_up, w_down,
+                 tg_buf, gg_buf, ug_buf, dg_buf,
+                 xs, ct, dys, part, wide, d_raw, dgu, dgu_t, act, act_t, d_act,
+                 twin_in, total, x_in, y_in, z_in,
+                 tok_buf, route_buf, comb_buf,
+                 g_send, g_recv, s_send, s_recv, w_sem, i_sem):
+    rows, width = tok.shape
+    hid = d_raw.shape[0]
+    wpad = xs.shape[1]
+    hpad = d_act.shape[1]
+    blocks = hpad // 128
+    chunk = rows * 8
+    z, y, x, c = place()
+    t = x * 2 + c
+    along, over_y, over_x, twin = peers(depth)
+    above, below = (z * 2 + 2 + y, t), (z * 2 - 2 + y, t)
+    inward = (jnp.where(z == 0, 1, depth - 2) * 2 + y, t)
+    table = [line_order(depth, zz) for zz in range(depth)]
+
+    def plane(i):
+        if i == 0:
+            return z
+        value = 0
+        for zz in range(depth):
+            value = value + jnp.where(z == zz, table[zz][i], 0)
+        return value
+
+    planes = [plane(i) for i in range(depth)]
+
+    def block(p, dy, dx, dc=0):
+        yy, xx, cc = (1 - y if dy else y), (1 - x if dx else x), (1 - c if dc else c)
+        return (p * 2 + yy) * 4 + xx * 2 + cc
+
+    def at_rows(at, count=rows):
+        return pl.ds(pl.multiple_of(at * rows, rows), count)
+
+    bufs = (xs, ct)
+    counts = [0, 0]
+    apart, far_end = (), False
+    side_counts = [[0, 0], [0, 0]]
+    group = depth * 5
+
+    barrier = pltpu.get_barrier_semaphore()
+    for device in [*along, over_y, over_x, twin]:
+        pl.semaphore_signal(barrier, inc=1, device_id=device, device_id_type=MESH)
+    me = block(z, 0, 0)
+    inputs = [
+        pltpu.make_async_copy(src, dst, i_sem.at[k])
+        for k, (src, dst) in enumerate(
+            ((routes, route_buf), (comb, comb_buf), (tok, tok_buf), (cot, ct.at[at_rows(me)]))
+        )
+    ]
+    for copy in inputs:
+        copy.start()
+    for side in range(2):
+        for j in range(blocks):
+            live = min(128, hid - 128 * j)
+            if live < 128:
+                at = 256 * j + 128 * side
+                wide[at + live // 16 * 16 : at + 128, :] = jnp.zeros((128 - live // 16 * 16, width), jnp.bfloat16)
+    loads = [pltpu.make_async_copy(w_down.at[0], d_raw, w_sem.at[2 * blocks])]
+    for side, weight in ((0, w_gate), (1, w_up)):
+        for j in range(blocks):
+            live = min(128, hid - 128 * j)
+            loads.append(
+                pltpu.make_async_copy(
+                    weight.at[0, 128 * j : 128 * j + live],
+                    wide.at[256 * j + 128 * side : 256 * j + 128 * side + live],
+                    w_sem.at[2 * j + side],
+                )
+            )
+    for load in loads:
+        load.start()
+
+    for copy in inputs:
+        copy.wait()
+    lane = lax.broadcasted_iota(jnp.int32, (rows, 128), 1)
+    first_lane = width - (wpad - 128)
+    owner = lax.rem(lane - first_lane + experts, experts)
+    named = jnp.zeros((rows, 128), jnp.float32)
+    across = lax.broadcasted_iota(jnp.int32, (rows, rows), 1) == lax.broadcasted_iota(jnp.int32, (rows, rows), 0)
+    for k in range(routes.shape[0]):
+        chosen = jnp.sum(jnp.where(across, route_buf[k : k + 1, :], 0), axis=1, keepdims=True)
+        weight = jnp.sum(jnp.where(across, comb_buf[k : k + 1, :], 0.0), axis=1, keepdims=True)
+        named = named + jnp.where(chosen == owner, weight, 0.0)
+    high = named.astype(jnp.bfloat16).astype(jnp.float32)
+    mid = (named - high).astype(jnp.bfloat16).astype(jnp.float32)
+    low = named - high - mid
+    piece = jnp.where(lane < first_lane + experts, high, jnp.where(lane < first_lane + 2 * experts, mid, low))
+    piece = jnp.where(lane < first_lane + 3 * experts, piece, 0.0)
+    tail = jnp.concatenate(
+        [tok_buf[:, wpad - 128 : width].astype(jnp.float32), jnp.zeros((rows, wpad - width), jnp.float32)], axis=1
+    )
+    xs[at_rows(me), : wpad - 128] = tok_buf[:, : wpad - 128]
+    xs[at_rows(me), wpad - 128 :] = jnp.where(lane < first_lane, tail, piece).astype(jnp.bfloat16)
+    pl.semaphore_wait(barrier, depth + 2)
+
+    def send(q, at, device):
+        copy = pltpu.make_async_remote_copy(
+            src_ref=bufs[q].at[at_rows(at)],
+            dst_ref=bufs[q].at[at_rows(at)],
+            send_sem=g_send.at[q, counts[q] // group],
+            recv_sem=g_recv.at[q, at],
+            device_id=device,
+            device_id_type=MESH,
+        )
+        counts[q] += 1
+        copy.start()
+
+    def landed(q, at):
+        pltpu.make_async_remote_copy(
+            src_ref=bufs[q].at[at_rows(at)],
+            dst_ref=bufs[q].at[at_rows(at)],
+            send_sem=g_send.at[q, 0],
+            recv_sem=g_recv.at[q, at],
+            device_id=twin,
+            device_id_type=MESH,
+        ).wait_recv()
+
+    def send_z(q, i, at):
+        if i == 0:
+            for device in (inward,) if far_end else (above, below):
+                send(q, at, device)
+        elif not far_end:
+            send(q, at, (jnp.where(planes[i] < z, z + 1, z - 1) * 2 + y, t))
+
+    def first_z(i, q):
+        at = block(planes[i], 0, 0)
+        if i:
+            landed(q, at)
+        send_z(q, i, at)
+        send(q, at, twin)
+
+    def first_xy(i, q):
+        at = block(planes[i], 0, 0)
+        send(q, at, over_x)
+        send(q, at, over_y)
+
+    def first(i, q):
+        first_z(i, q)
+        first_xy(i, q)
+
+    def second(i, q):
+        by_y, by_x = block(planes[i], 1, 0), block(planes[i], 0, 1)
+        near, far, onward = (by_x, by_y, over_y) if q else (by_y, by_x, over_x)
+        landed(q, near)
+        if i == 0 or apart[i] > ZREACH:
+            send(q, near, onward)
+        send(q, near, twin)
+        landed(q, far)
+        send(q, far, twin)
+
+    def third(i, q):
+        at = block(planes[i], 1, 1)
+        landed(q, at)
+        if apart[i] < ZREACH:
+            send_z(q, i, at)
+        send(q, at, twin)
+
+    def prepare():
+        for load in loads:
+            load.wait()
+        d_act[...] = jnp.zeros(d_act.shape, jnp.float32)
+
+    def here_of(i):
+        return pl.ds(pl.multiple_of(planes[i] * chunk, chunk), chunk)
+
+    def scales(i, k):
+        for q in range(2):
+            landed(q, block(planes[i], k // 2, k % 2, 1))
+        first_row = block(planes[i], k // 2, k % 2) - c
+        here = at_rows(first_row, 2 * rows)
+        spot = lax.broadcasted_iota(jnp.int32, (2 * rows, 128), 1) - first_lane
+        e = lax.axis_index("expert")
+        mine = (spot == e) | (spot == e + experts) | (spot == e + 2 * experts)
+        scale = jnp.sum(jnp.where(mine, xs[here, wpad - 128 :].astype(jnp.float32), 0.0), axis=1, keepdims=True)
+        dys[here, :] = (scale * ct[here, :].astype(jnp.float32)).astype(jnp.bfloat16)
+
+    def acts(i):
+        d_act[:, :hid] = contract_cols(dys[here_of(i), :], d_raw[...])
+
+    def gates(i):
+        here = here_of(i)
+        for j in range(blocks):
+            both = contract_cols(xs[here, :width], wide[256 * j : 256 * j + 256, :])
+            gate, upper = both[:, :128], both[:, 128:]
+            da = d_act[:, 128 * j : 128 * j + 128]
+            sigma = jax.nn.sigmoid(gate)
+            act[here, 128 * j : 128 * j + 128] = (gate * sigma * upper).astype(jnp.bfloat16)
+            dgate = da * upper * sigma * (1.0 + gate * (1.0 - sigma))
+            dupper = da * gate * sigma
+            dgu[here, 256 * j : 256 * j + 128] = dgate.astype(jnp.bfloat16)
+            dgu[here, 256 * j + 128 : 256 * j + 256] = dupper.astype(jnp.bfloat16)
+
+    def backs(i, w):
+        here = here_of(i)
+        for start in range(sides_of[w].start, sides_of[w].stop, 512):
+            cols = slice(start, min(start + 512, width))
+            part[here, cols] = jnp.dot(
+                dgu[here, :], wide[:, cols], preferred_element_type=jnp.float32
+            ).astype(jnp.bfloat16)
+
+    def turns(i):
+        here = here_of(i)
+        for j in range(blocks):
+            act_t[128 * j : 128 * j + 128, here] = act[here, 128 * j : 128 * j + 128].T
+        for j in range(2 * blocks):
+            dgu_t[128 * j : 128 * j + 128, here] = dgu[here, 128 * j : 128 * j + 128].T
+
+    half = rows // 2
+    halves = [pl.ds(0, half), pl.ds(half, half)]
+    cut = pad_to(width // 2, 512)
+    sides_of = (slice(0, cut), slice(cut, width)) if SPLIT else (slice(0, width),)
+
+    def ssend(src, dst, device, w, recv, level=1):
+        copy = pltpu.make_async_remote_copy(
+            src_ref=src,
+            dst_ref=dst,
+            send_sem=s_send.at[w, level],
+            recv_sem=s_recv.at[w * per_side + recv],
+            device_id=device,
+            device_id_type=MESH,
+        )
+        copy.start()
+        return copy
+
+    def add(a, b):
+        return (a.astype(jnp.float32) + b.astype(jnp.float32)).astype(jnp.bfloat16)
+
+    def both(stage):
+        return lambda i, *w: [stage(i, k) for k in (w or range(len(sides_of)))]
+
+    corners = ((1, 1), (0, 1), (1, 0), (0, 0))
+    over, last = {}, {}
+    z_base = depth * 7
+    per_side = depth * 9
+
+    def s0(i, w):
+        cols = sides_of[w]
+        for dy, dx in corners:
+            k = i * 4 + dy * 2 + dx
+            ssend(part.at[at_rows(block(planes[i], dy, dx, 1)), cols], twin_in.at[k, :, cols], twin, w, i, 0)
+
+    def merge(h, i, other, w):
+        over[h, i, other, w].wait_recv()
+        cols = sides_of[w]
+        if h == 0:
+            k, got = i * 4 + other * 2, x_in[i * 2 + other, :, cols]
+        else:
+            k, got = i * 4 + other, y_in[i * 2 + other, :, cols]
+        total[k, halves[h], cols] = add(total[k, halves[h], cols], got)
+        return k
+
+    def s1(i, w):
+        cols, base = sides_of[w], depth
+        span = twin_in.at[i * 4 : i * 4 + 4, :, cols]
+        pltpu.make_async_remote_copy(
+            src_ref=span,
+            dst_ref=span,
+            send_sem=s_send.at[w, 0],
+            recv_sem=s_recv.at[w * per_side + i],
+            device_id=twin,
+            device_id_type=MESH,
+        ).wait_recv()
+        for dy, dx in corners:
+            k = i * 4 + dy * 2 + dx
+            total[k, :, cols] = add(part[at_rows(block(planes[i], dy, dx)), cols], twin_in[k, :, cols])
+            if dx:
+                at = i * 2 + dy
+                over[0, i, dy, w] = ssend(
+                    total.at[k, halves[0], cols], x_in.at[at, :, cols], over_x, w, base + at
+                )
+            if dy:
+                at = i * 2 + dx
+                over[1, i, dx, w] = ssend(
+                    total.at[k, halves[1], cols], y_in.at[at, :, cols], over_y, w, base + depth * 2 + at
+                )
+
+    def s2(i, w):
+        cols, base, at = sides_of[w], depth * 5, depth * 2 + i
+        k = merge(0, i, 1, w)
+        last[0, i, w] = ssend(total.at[k, halves[0], cols], y_in.at[at, :, cols], over_y, w, base + i)
+        k = merge(1, i, 1, w)
+        last[1, i, w] = ssend(total.at[k, halves[1], cols], x_in.at[at, :, cols], over_x, w, base + depth + i)
+
+    def s3(i, w):
+        cols = sides_of[w]
+        for h in range(2):
+            k = merge(h, i, 0, w)
+            last[h, i, w].wait_recv()
+            got = (x_in if h else y_in)[depth * 2 + i, :, cols]
+            total[k, halves[h], cols] = add(total[k, halves[h], cols], got)
+            if i:
+                ssend(
+                    total.at[k, halves[h], cols],
+                    z_in.at[h * depth + z, :, cols],
+                    (planes[i] * 2 + y, t),
+                    w,
+                    z_base + h * depth + z,
+                )
+
+    def finish(w):
+        cols = sides_of[w]
+        for h in range(2):
+            value = total[0, halves[h], cols].astype(jnp.float32)
+            for step in range(1, depth):
+                at = h * depth + lax.rem(z + step, depth)
+                pltpu.make_async_remote_copy(
+                    src_ref=total.at[0, halves[h], cols],
+                    dst_ref=z_in.at[at, :, cols],
+                    send_sem=s_send.at[w, 1],
+                    recv_sem=s_recv.at[w * per_side + z_base + at],
+                    device_id=twin,
+                    device_id_type=MESH,
+                ).wait_recv()
+                value = value + z_in[at, :, cols].astype(jnp.float32)
+            tg_buf[halves[h], cols] = value.astype(jnp.bfloat16)
+
+    msize = 256
+    mfull, mrest = tiles(width, msize)
+
+    def wide_tile(cols):
+        out = jnp.dot(dgu_t[...], xs[:, cols], preferred_element_type=jnp.float32)
+        for j in range(blocks):
+            live = min(128, hid - 128 * j)
+            for buf, side in ((gg_buf, 0), (ug_buf, 1)):
+                at = 256 * j + 128 * side
+                buf[128 * j : 128 * j + live, cols] = out[at : at + live].astype(jnp.bfloat16)
+
+    def wide_grads(lo, hi):
+        def body(k, _):
+            wide_tile(pl.ds(pl.multiple_of(k * msize, msize), msize))
+            return 0
+
+        lax.fori_loop(lo, hi, body, 0)
+
+    def wides(k):
+        lo, hi = k * mfull // 4, (k + 1) * mfull // 4
+        wide_grads(lo, hi)
+        if k == 3 and mrest:
+            wide_tile(slice(mfull * msize, width))
+
+    nsize = 512
+    nfull, nrest = tiles(width, nsize)
+
+    def down():
+        def body(k, _):
+            cols = pl.ds(pl.multiple_of(k * nsize, nsize), nsize)
+            dg_buf[:, cols] = jnp.dot(
+                act_t[...], dys[:, cols], preferred_element_type=jnp.float32
+            )[:hid].astype(jnp.bfloat16)
+            return 0
+
+        lax.fori_loop(0, nfull, body, 0)
+        if nrest:
+            dg_buf[:, nfull * nsize : width] = jnp.dot(
+                act_t[...], dys[:, nfull * nsize : width], preferred_element_type=jnp.float32
+            )[:hid].astype(jnp.bfloat16)
+
+    edge = (z == 0) | (z == depth - 1)
+    sides = ((edge, tuple(range(depth)), True), (jnp.logical_not(edge), tuple(abs(p - 1) for p in table[1]), False))
+
+    def drain():
+        def leave(counts):
+            for q in range(2):
+                for k in range(0, counts[q], group):
+                    span = bufs[q].at[pl.ds(0, min(group, counts[q] - k) * rows)]
+                    pltpu.make_async_remote_copy(
+                        src_ref=span,
+                        dst_ref=span,
+                        send_sem=g_send.at[q, k // group],
+                        recv_sem=g_recv.at[q, 0],
+                        device_id=twin,
+                        device_id_type=MESH,
+                    ).wait_send()
+
+        for k in range(2):
+            pl.when(sides[k][0])(functools.partial(leave, side_counts[k]))
+        for w in range(len(sides_of)):
+            for k, span in enumerate((twin_in.at[:, :, sides_of[w]], total.at[: depth * 4 - 1, :, sides_of[w]])):
+                pltpu.make_async_remote_copy(
+                    src_ref=span,
+                    dst_ref=span,
+                    send_sem=s_send.at[w, k],
+                    recv_sem=s_recv.at[0],
+                    device_id=twin,
+                    device_id_type=MESH,
+                ).wait_send()
+
+    stages = {
+        "1": first, "2": second, "3": third, "5": first_z, "6": first_xy, "p": prepare, "c": scales, "a": acts, "g": gates,
+        "b": both(backs), "s": both(s0), "t": both(s1), "u": both(s2), "v": both(s3), "d": down, "w": wides, "f": finish, "x": turns,
+    }
+
+    def walk(steps):
+        for step in steps:
+            with jax.named_scope(step):
+                stages[step[0]](*[int(k) for k in step[1:]])
+
+    def walk_side(k, steps):
+        nonlocal apart, far_end
+        cond, apart, far_end = sides[k]
+        counts[:] = side_counts[k]
+        pl.when(cond)(lambda: walk(steps))
+        side_counts[k] = counts[:]
+
+    for steps in PLAN:
+        if isinstance(steps[0], tuple):
+            for k in range(2):
+                walk_side(k, steps[k])
+        else:
+            walk(steps)
+    with jax.named_scope("drain"):
+        drain()
+
+
+PLAN = (
+    (
+        ("100", "101",),
+        ("100", "101",),
+    ),
+    ("p",),
+    (
+        ("200", "110", "201", "111",),
+        ("200", "510", "520", "610", "201", "511", "521", "611", "620", "621",),
+    ),
+    ("c00", "c01", "c02",),
+    (
+        ("300", "120", "301", "121",),
+        ("530", "531", "300", "301", "630", "631",),
+    ),
+    ("c03", "a0", "g0", "b0", "s0", "x0",),
+    (
+        ("210", "211", "130", "131", "310", "311", "220", "221",),
+        ("310", "311", "320", "321", "210", "211",),
+    ),
+    ("c10", "c11", "c12", "c13", "t0", "a1", "g1", "b1", "s1", "x1",),
+    (
+        ("230", "231", "320", "321",),
+        ("220", "221", "330", "331",),
+    ),
+    ("c20", "c21", "c22", "c23", "u0", "t1", "a2", "g2",),
+    (
+        ("330", "331",),
+        ("230", "231",),
+    ),
+    ("b2", "s2", "x2",),
+    ("c30", "c31", "c32", "c33", "v0", "u1", "t2", "a3", "g3", "v1", "b3", "s3", "u2", "x3"),
+    ("t3", "d", "v2", "u3", "w0", "w1", "v3", "w2", "w3", "f0"),
+)
+ZREACH = 2
+SPLIT = 0
+VMEM_LIMIT = 54 * 1024 * 1024
+
+
+def settle_kernel(*refs):
+    count = len(refs) // 2
+    moves = [
+        pltpu.make_async_copy(src, dst, refs[-1].at[k])
+        for k, (src, dst) in enumerate(zip(refs[:count], refs[count : 2 * count]))
+    ]
+    for move in moves:
+        move.start()
+    for move in moves:
+        move.wait()
+
+
+def settle(*arrays):
+    return pl.pallas_call(
+        settle_kernel,
+        out_shape=[jax.ShapeDtypeStruct(a.shape, a.dtype) for a in arrays],
+        in_specs=[pl.BlockSpec(memory_space=pltpu.VMEM)] * len(arrays),
+        out_specs=[pl.BlockSpec(memory_space=pl.ANY)] * len(arrays),
+        scratch_shapes=[pltpu.SemaphoreType.DMA((len(arrays),))],
+        compiler_params=pltpu.CompilerParams(vmem_limit_bytes=8 * 1024 * 1024),
+    )(*arrays)
+
+
+def fused(tokens, cotangent, routes, combine, w_gate, w_up, w_down):
+    rows, width = tokens.shape
+    hid = w_gate.shape[2]
+    groups = lax.axis_size("expert")
+    depth = groups // 2
+    wpad, hpad = pad_to(width, 128), pad_to(hid, 128)
+    count = groups * 4
+    everyone = count * rows
+    half = rows // 2
+    vmem = pl.BlockSpec(memory_space=pltpu.VMEM)
+    hbm = pl.BlockSpec(memory_space=pl.ANY)
+    bf16, f32 = jnp.bfloat16, jnp.float32
+    token_grad, gate_t, up_t, down = pl.pallas_call(
+        lambda *refs: fused_kernel(depth, groups, *refs),
+        out_shape=[
+            pltpu.VMEM(tokens.shape, bf16),
+            pltpu.VMEM((hid, width), bf16),
+            pltpu.VMEM((hid, width), bf16),
+            pltpu.VMEM((hid, width), bf16),
+        ],
+        in_specs=[hbm] * 7,
+        out_specs=[vmem] * 4,
+        scratch_shapes=[
+            pltpu.VMEM((everyone, wpad), bf16),
+            pltpu.VMEM((everyone, width), bf16),
+            pltpu.VMEM((everyone, width), bf16),
+            pltpu.VMEM((everyone, width), bf16),
+            pltpu.VMEM((2 * hpad, width), bf16),
+            pltpu.VMEM((hid, width), bf16),
+            pltpu.VMEM((everyone, 2 * hpad), bf16),
+            pltpu.VMEM((2 * hpad, everyone), bf16),
+            pltpu.VMEM((everyone, hpad), bf16),
+            pltpu.VMEM((hpad, everyone), bf16),
+            pltpu.VMEM((rows * 8, hpad), f32),
+            pltpu.VMEM((depth * 4, rows, width), bf16),
+            pltpu.VMEM((depth * 4, rows, width), bf16),
+            pltpu.VMEM((depth * 3, half, width), bf16),
+            pltpu.VMEM((depth * 3, half, width), bf16),
+            pltpu.VMEM((depth * 2, half, width), bf16),
+            pltpu.VMEM(tokens.shape, bf16),
+            pltpu.VMEM(routes.shape[::-1], jnp.int32),
+            pltpu.VMEM(combine.shape[::-1], f32),
+            pltpu.SemaphoreType.DMA((2, 2)),
+            pltpu.SemaphoreType.DMA((2, count)),
+            pltpu.SemaphoreType.DMA((1 + SPLIT, 2)),
+            pltpu.SemaphoreType.DMA(((1 + SPLIT) * depth * 9,)),
+            pltpu.SemaphoreType.DMA((hpad // 64 + 1,)),
+            pltpu.SemaphoreType.DMA((4,)),
+        ],
+        compiler_params=pltpu.CompilerParams(
+            collective_id=0, has_side_effects=True, vmem_limit_bytes=VMEM_LIMIT
+        ),
+    )(
+        tokens,
+        cotangent,
+        routes.T,
+        combine.T,
+        jnp.swapaxes(w_gate, 1, 2),
+        jnp.swapaxes(w_up, 1, 2),
+        w_down,
+    )
+    token_grad, gate_t, up_t, down = settle(token_grad, gate_t, up_t, down)
+    return token_grad, jnp.swapaxes(gate_t, 0, 1)[None], jnp.swapaxes(up_t, 0, 1)[None], down[None]
+
+
 def on_device(tokens, cotangent, routes, combine, w_gate, w_up, w_down):
     groups, shards = lax.axis_size("expert"), lax.axis_size("tensor")
     rows, top_count = routes.shape
     few = w_gate.shape[0] == 1 and groups <= 2 * top_count
-    plan = dense if few and shards == 4 and groups % 2 == 0 and rows % 32 == 0 else slotted
+    plan = slotted
+    if few and shards == 4 and groups % 2 == 0 and rows % 32 == 0:
+        plan = fused if groups == 8 and -tokens.shape[1] % 128 >= 3 * groups else dense
     return plan(tokens, cotangent, routes, combine, w_gate, w_up, w_down)
 
 

time: 181 us -> 88.9 us (0.49)
  matrix products: 39.8 us -> 0 us
  Pallas kernels: 118 us -> 87.9 us
  local copies, waits for them, and re-layouts: 14.1 us -> 0 us
  other arithmetic: 8.02 us -> 0 us
    dot_general x8 -> x0, matrix products: 39.8 us -> none  [the longest x3 17.9 us: contract_rows(): lax.dot_general(left, right, (((0,), (0,)), ((), ())), preferred_element_...]
    pallas_call x2, Pallas kernels: 118 us -> 87.9 us  [the longest x1 85.1 us: fused(): pl.pallas_call(lambda *refs: fused_kernel(depth, groups, *refs), out_shap...]
    convert_element_type x1 -> x0, local copies, waits for them, and re-layouts: 8.52 us -> none  [dense(): token_grad = scatter_sum(part.astype(jnp.bfloat16), rows)]
    convert_element_type x2 -> x0, other arithmetic: 6.57 us -> none  [dense(): (scale * cot.reshape(-1, width).astype(jnp.float32)).astype(jnp.bfloat16)]
    unnamed x23 -> x0, local copies, waits for them, and re-layouts: 3.43 us -> none
    dynamic_slice x2 -> x0, local copies, waits for them, and re-layouts: 2.12 us -> none  [dense(): lax.dynamic_slice_in_dim(table, lax.axis_index('expert'), 1, axis=1)]
where the time goes in v2:
time: 88.9 us; the launch traced here: 88.7 us
  Pallas kernels  87.9 us (99%)
    pallas_call x1, Pallas kernels, fused(): pl.pallas_call(lambda *refs: fused_kernel(depth, groups, *refs), out_shap...  85.1 us
    pallas_call x1, Pallas kernels, settle(): pl.pallas_call(settle_kernel, out_shape=[jax.ShapeDtypeStruct(a.shape, a....  2.82 us

profile of v2, /device:TPU:0, one launch (start us, length us, event | category | flops | bytes accessed | tf_op | source)
XLA Modules:
  0.0 88.7 jit_solution(12011681610832613853)
XLA Ops:
  0.6 85.1 %shard_map.102 = (bf16[32,2880]{1,0:T(8,128)(2,1)S(1)}, bf16[360,2880]{1,0:T(8,128)(2,1)S(1)}, bf16[360,2880]{1,0:T(8,128)(2,1)S(1)}, bf16[360,2880]{1,0:T(8,128)(2,1)S(1)}) custom-call(bf16[32,2880]{1,0:T(8,128)(2,1)} %refs_0_.1, bf16[32,2880]{1,0:T(8,128)(2,1)} %refs_1_.1, s32[4,32]{1,0:T(4,128)} %bitcast.13, f32[4,32]{1,0:T(4,128)} %bitcast.14, ...), custom_call_target="tpu_custom_call" | custom-call | tf_op jit(solution)/shard_map/pallas_call | solution.py:858
  85.7 2.8 %shard_map.103 = (bf16[32,2880]{1,0:T(8,128)(2,1)}, bf16[360,2880]{1,0:T(8,128)(2,1)}, bf16[360,2880]{1,0:T(8,128)(2,1)}, bf16[360,2880]{1,0:T(8,128)(2,1)}) custom-call(bf16[32,2880]{1,0:T(8,128)(2,1)S(1)} %get-tuple-element.12.refs_0_, bf16[360,2880]{1,0:T(8,128)(2,1)S(1)} %get-tuple-element.13.refs_1_, bf16[360,2880]{1,0:T(8,128)(2,1)S(1)} %get-tuple-element.14.refs_2_, ...), custom_call_target="tpu_custom_call" | custom-call | tf_op jit(solution)/shard_map/pallas_call | solution.py:836

commit v3 on v2

--- a/solution.py
+++ b/solution.py
@@ -812,7 +812,7 @@
         ("230", "231",),
     ),
     ("b2", "s2", "x2",),
-    ("c30", "c31", "c32", "c33", "v0", "u1", "t2", "a3", "g3", "v1", "b3", "s3", "u2", "x3"),
+    ("c30", "c31", "c32", "c33", "v0", "u1", "t2", "a3", "g3", "b3", "s3", "v1", "u2", "x3"),
     ("t3", "d", "v2", "u3", "w0", "w1", "v3", "w2", "w3", "f0"),
 )
 ZREACH = 2

time: 88.9 us -> 87.5 us (0.984)
  Pallas kernels: 87.9 us -> 86.6 us
    pallas_call x1, Pallas kernels: 85.1 us -> 83.7 us  [fused(): pl.pallas_call(lambda *refs: fused_kernel(depth, groups, *refs), out_shap...]
where the time goes in v3:
time: 87.5 us; the launch traced here: 87.4 us
  Pallas kernels  86.6 us (99%)
    pallas_call x1, Pallas kernels, fused(): pl.pallas_call(lambda *refs: fused_kernel(depth, groups, *refs), out_shap...  83.7 us
    pallas_call x1, Pallas kernels, settle(): pl.pallas_call(settle_kernel, out_shape=[jax.ShapeDtypeStruct(a.shape, a....  2.82 us

profile of v3, /device:TPU:0, one launch (start us, length us, event | category | flops | bytes accessed | tf_op | source)
XLA Modules:
  0.0 87.4 jit_solution(1238641140222014229)
XLA Ops:
  0.6 83.7 %shard_map.102 = (bf16[32,2880]{1,0:T(8,128)(2,1)S(1)}, bf16[360,2880]{1,0:T(8,128)(2,1)S(1)}, bf16[360,2880]{1,0:T(8,128)(2,1)S(1)}, bf16[360,2880]{1,0:T(8,128)(2,1)S(1)}) custom-call(bf16[32,2880]{1,0:T(8,128)(2,1)} %refs_0_.1, bf16[32,2880]{1,0:T(8,128)(2,1)} %refs_1_.1, s32[4,32]{1,0:T(4,128)} %bitcast.13, f32[4,32]{1,0:T(4,128)} %bitcast.14, ...), custom_call_target="tpu_custom_call" | custom-call | tf_op jit(solution)/shard_map/pallas_call | solution.py:858
  84.4 2.8 %shard_map.103 = (bf16[32,2880]{1,0:T(8,128)(2,1)}, bf16[360,2880]{1,0:T(8,128)(2,1)}, bf16[360,2880]{1,0:T(8,128)(2,1)}, bf16[360,2880]{1,0:T(8,128)(2,1)}) custom-call(bf16[32,2880]{1,0:T(8,128)(2,1)S(1)} %get-tuple-element.12.refs_0_, bf16[360,2880]{1,0:T(8,128)(2,1)S(1)} %get-tuple-element.13.refs_1_, bf16[360,2880]{1,0:T(8,128)(2,1)S(1)} %get-tuple-element.14.refs_2_, ...), custom_call_target="tpu_custom_call" | custom-call | tf_op jit(solution)/shard_map/pallas_call | solution.py:836
